TPU v7x, 16 devices: a whole 2x2x2 slice. The times are simulated.
16 devices in a mesh: dp: 4 (over z, y), tp: 4 (over x, core).
Axes of the slice: x: 2, y: 2, z: 2, core: 2. Of those that a mesh axis runs over, the one named last changes fastest.
Arguments:
- tokens: bfloat16 [8, 128, 5120], P('dp'), parts along dimension 0
- seq_lens: int32 [8], P('dp'), parts along dimension 0
- w_q: bfloat16 [5120, 5120], P(None, 'tp')
- w_k: bfloat16 [5120, 5120], P(None, 'tp')
- w_v: bfloat16 [5120, 5120], P(None, 'tp')
- w_o: bfloat16 [5120, 5120], P('tp')
- g_q: bfloat16 [5120], P('tp')
- g_k: bfloat16 [5120], P('tp')
- g_attn: bfloat16 [5120], replicated
- g_mlp: bfloat16 [5120], replicated
- w_gate: bfloat16 [5120, 13824], P(None, 'tp')
- w_up: bfloat16 [5120, 13824], P(None, 'tp')
- w_down: bfloat16 [13824, 5120], P('tp')
Outputs:
- output 1: bfloat16 [8, 128, 5120], P('dp'), parts along dimension 0
- output 2: bfloat16 [8, 40, 128, 128], P('dp', 'tp'), parts along dimension 0
- output 3: bfloat16 [8, 40, 128, 128], P('dp', 'tp'), parts along dimension 0
There are 4 independent parts. A program takes and returns all parts, laid end to end along the dimension named above; an argument that names none is the same for every part.
All inputs are finite; a program needn't handle non-finite values.
Results may differ from a plain program's by a relative error of at most 0.0163826.
Values are sent between devices in bfloat16 or wider.
A program may use at most 1 GiB of HBM per device.

v0:
```python
import jax
import jax.numpy as jnp
from jax import lax
from jax.sharding import PartitionSpec as P

HEAD_DIM = 128
ROPE_BASE = 500000.0
NORM_EPS = 1e-6


def rope_tables(seq_len, head_dim):
    half_dim = head_dim // 2
    inv_freq = ROPE_BASE ** (-2.0 * jnp.arange(half_dim, dtype=jnp.float32) / head_dim)
    angles = jnp.arange(seq_len, dtype=jnp.float32)[:, None] * inv_freq[None, :]
    angles = jnp.concatenate([angles, angles], axis=-1)
    return jnp.cos(angles), jnp.sin(angles)


def apply_rope(vecs, cos_tab, sin_tab, head_axes):
    half_dim = vecs.shape[-1] // 2
    table_shape = (cos_tab.shape[0],) + (1,) * head_axes + (cos_tab.shape[1],)
    rotated = jnp.concatenate([-vecs[..., half_dim:], vecs[..., :half_dim]], axis=-1)
    return vecs * cos_tab.reshape(table_shape) + rotated * sin_tab.reshape(table_shape)


def rms_scale(vals):
    return lax.rsqrt(jnp.mean(vals * vals, axis=-1, keepdims=True) + NORM_EPS)


def post_norm(base, branch, gain):
    branch32 = branch.astype(jnp.float32)
    return (base.astype(jnp.float32) + branch32 * rms_scale(branch32) * gain.astype(jnp.float32)).astype(jnp.bfloat16)


def solution(mesh):
    tp_size = mesh.shape['tp']

    def local_layer(tokens, seq_lens, w_q, w_k, w_v, w_o, g_q, g_k, g_attn, g_mlp, w_gate, w_up, w_down):
        prompts, seq_len = tokens.shape[0], tokens.shape[1]
        kv_local = w_k.shape[1] // HEAD_DIM
        group_size = w_q.shape[1] // w_k.shape[1]
        q_raw = jnp.einsum('bsd,dn->bsn', tokens, w_q, preferred_element_type=jnp.float32)
        k_raw = jnp.einsum('bsd,dn->bsn', tokens, w_k, preferred_element_type=jnp.float32)
        v_new = jnp.einsum('bsd,dn->bsn', tokens, w_v, preferred_element_type=jnp.float32).astype(jnp.bfloat16)
        q_sumsq = lax.psum(jnp.sum(q_raw * q_raw, axis=-1, keepdims=True), 'tp')
        k_sumsq = lax.psum(jnp.sum(k_raw * k_raw, axis=-1, keepdims=True), 'tp')
        q_norm = q_raw * lax.rsqrt(q_sumsq / (w_q.shape[1] * tp_size) + NORM_EPS) * g_q.astype(jnp.float32)
        k_norm = k_raw * lax.rsqrt(k_sumsq / (w_k.shape[1] * tp_size) + NORM_EPS) * g_k.astype(jnp.float32)
        cos_tab, sin_tab = rope_tables(seq_len, HEAD_DIM)
        queries = apply_rope(q_norm.reshape(prompts, seq_len, kv_local, group_size, HEAD_DIM), cos_tab, sin_tab, 2).astype(jnp.bfloat16)
        keys_new = apply_rope(k_norm.reshape(prompts, seq_len, kv_local, HEAD_DIM), cos_tab, sin_tab, 1).astype(jnp.bfloat16)
        k_cache = jnp.transpose(keys_new, (0, 2, 1, 3))
        v_cache = jnp.transpose(v_new.reshape(prompts, seq_len, kv_local, HEAD_DIM), (0, 2, 1, 3))
        scores = jnp.einsum('bsgrd,bgtd->bgrst', queries, k_cache, preferred_element_type=jnp.float32) * HEAD_DIM ** -0.5
        positions = jnp.arange(seq_len)
        allowed = (positions[None, None, :] <= positions[None, :, None]) & (positions[None, None, :] < seq_lens[:, None, None])
        scores = jnp.where(allowed[:, None, None], scores, -1e30)
        attn_probs = jax.nn.softmax(scores, axis=-1).astype(jnp.bfloat16)
        attn_out = jnp.einsum('bgrst,bgtd->bsgrd', attn_probs, v_cache, preferred_element_type=jnp.float32).astype(jnp.bfloat16)
        attn_part = jnp.einsum('bsn,nd->bsd', attn_out.reshape(prompts, seq_len, -1), w_o, preferred_element_type=jnp.float32).astype(jnp.bfloat16)
        attn_proj = lax.psum(attn_part, 'tp')
        hidden = post_norm(tokens, attn_proj, g_attn)
        gate_pre = jnp.einsum('bsd,df->bsf', hidden, w_gate, preferred_element_type=jnp.float32)
        up_proj = jnp.einsum('bsd,df->bsf', hidden, w_up, preferred_element_type=jnp.float32)
        act_out = (jax.nn.silu(gate_pre) * up_proj).astype(jnp.bfloat16)
        mlp_part = jnp.einsum('bsf,fd->bsd', act_out, w_down, preferred_element_type=jnp.float32).astype(jnp.bfloat16)
        mlp_out = lax.psum(mlp_part, 'tp')
        out_hidden = post_norm(hidden, mlp_out, g_mlp)
        return out_hidden, k_cache, v_cache

    return jax.shard_map(local_layer, mesh=mesh, in_specs=(P('dp', None, None), P('dp'), P(None, 'tp'), P(None, 'tp'), P(None, 'tp'), P('tp', None), P('tp'), P('tp'), P(), P(), P(None, 'tp'), P(None, 'tp'), P('tp', None)), out_specs=(P('dp', None, None), P('dp', 'tp', None, None), P('dp', 'tp', None, None)), check_vma=False)
```

profile of v0, /device:TPU:0, one launch (start us, length us, event | category | flops | bytes accessed | tf_op | source)
XLA Modules:
  0.0 237.0 jit_solution(12012255056200539477)
XLA Ops:
  7.2 0.0 all-reduce.4.cloned.1.call-start
  7.2 0.0 copy-start.5
  7.3 0.0 copy-start.12
  7.3 9.9 %multiply_reduce_fusion.1 = (f32[2,128]{1,0:T(2,128)S(1)}, f32[2,128,1280]{2,1,0:T(8,128)S(1)}) fusion(bf16[2,128,5120]{2,1,0:T(8,128)(2,1)} %param.13, bf16[5120,1280]{1,0:T(8,128)(2,1)} %param.16), kind=kOutput, calls=%fused_computation.48 | convolution fusion | flops 3356098304 | bytes 17040384 | tf_op jit(solution)/shard_map/bsd,dn->bsn/dot_general | solution.py:43
  17.2 0.0 copy-done.5
  17.2 0.0 copy-done.12
  17.3 0.0 copy-start.10
  17.3 4.6 %multiply_reduce_fusion = (f32[2,128]{1,0:T(2,128)S(1)}, f32[2,128,1280]{2,1,0:T(8,128)}) fusion(bf16[2,128,5120]{2,1,0:T(8,128)(2,1)S(1)} %copy-done.5, bf16[5120,1280]{1,0:T(8,128)(2,1)S(1)} %copy-done.12), kind=kOutput, calls=%fused_computation.46 | convolution fusion | flops 3356098304 | bytes 17040384 | tf_op jit(solution)/shard_map/bsd,dn->bsn/dot_general | solution.py:42
  21.9 0.0 copy-done.10
  21.9 8.6 %all-reduce = (f32[2,128,1]{1,0,2:T(2,128)S(1)}, f32[2,128,1]{1,0,2:T(2,128)S(1)}) all-reduce(f32[2,128,1]{1,0,2:T(2,128)S(1)} %bitcast.84, f32[2,128,1]{1,0,2:T(2,128)S(1)} %bitcast.85), channel_id=1, replica_groups=mesh['dp'=4,'tp'=4] {'tp'}, use_global_device_ids=true, to_apply=%region_1.0 | all-reduce | flops 512 | bytes 4096 | tf_op jit(solution)/shard_map/psum | solution.py:46
  30.5 0.2 multiply_multiply_fusion.1
  30.7 0.0 copy-start.11
  30.7 0.4 copy.27
  31.1 0.0 copy-start.7
  31.1 1.1 slice_negate_fusion.1
  32.3 0.1 iota_multiply_fusion
  32.4 0.2 fusion.57
  32.6 0.0 copy-done.11
  32.6 0.3 copy-done.7
  32.9 1.2 multiply_multiply_fusion
  34.2 0.0 copy-start.13
  34.2 1.7 copy.28
  35.9 0.0 copy-start.6
  35.9 1.1 fusion.51
  37.0 0.0 copy-done.13
  37.0 0.1 iota_compare_fusion.1
  37.1 1.0 copy-done.6
  38.1 6.7 %fusion.38 = bf16[2,128,1280]{2,1,0:T(8,128)(2,1)S(1)} fusion(bf16[2,128,5120]{2,1,0:T(8,128)(2,1)S(1)} %copy-done.6, bf16[5120,1280]{1,0:T(8,128)(2,1)} %param.17), kind=kOutput, calls=%fused_computation.32 | convolution fusion | flops 3355770880 | bytes 16384000 | tf_op jit(solution)/shard_map/bsd,dn->bsn/dot_general | solution.py:44
  44.8 1.1 copy.26
  45.9 0.0 copy-start.2
  45.9 0.0 copy-start.3
  45.9 0.1 broadcast_and_fusion
  46.0 1.6 fusion.50
  47.6 0.0 copy-done.2
  47.6 0.0 copy-done.3
  47.6 0.0 copy-start.4
  47.6 0.5 fusion.60
  48.1 0.2 fusion.48
  48.3 0.3 copy-done.4
  48.7 0.4 convolution_convert_fusion
  49.0 9.7 %fusion.17 = bf16[2,128,5120]{2,1,0:T(8,128)(2,1)} fusion(bf16[2,128,1280]{1,2,0:T(8,128)(2,1)S(1)} %bitcast.83, bf16[1280,5120]{1,0:T(8,128)(2,1)} %param.18), kind=kOutput, calls=%fused_computation.19 | convolution fusion | flops 3356753920 | bytes 16384000 | tf_op jit(solution)/shard_map/bsn,nd->bsd/dot_general | solution.py:60
  58.7 0.0 copy-start.8
  58.7 0.0 all-reduce.4.cloned.1.call-update
  58.8 0.2 all-reduce.6.cloned.1.call-start
  59.0 0.4 copy-done.8
  59.4 55.6 %all-reduce.4.cloned.1.call-done = bf16[2,128,5120]{2,1,0:T(8,128)(2,1)} async-done(((bf16[2,128,5120]{2,1,0:T(8,128)(2,1)}), bf16[2,128,5120]{2,1,0:T(8,128)(2,1)}) %all-reduce.4.cloned.1.call-update) | async-done | bytes 2621456 | tf_op jit(solution)/shard_map/psum | solution.py:61
  115.1 0.0 copy-start.1
  115.1 2.5 %fusion.23 = f32[2,128]{1,0:T(2,128)S(1)} fusion(bf16[2,128,5120]{2,1,0:T(8,128)(2,1)} %all-reduce.4.cloned.1.call-done), kind=kLoop, calls=%fused_computation.21 | loop fusion | flops 3931904 | bytes 2622464 | tf_op jit(solution)/shard_map/reduce_sum | solution.py:27
  117.6 0.0 copy-done.1
  117.6 3.1 %fusion.26 = bf16[2,128,5120]{2,1,0:T(8,128)(2,1)S(1)} fusion(bf16[2,128,5120]{2,1,0:T(8,128)(2,1)S(1)} %copy-done.1, bf16[2,128,5120]{2,1,0:T(8,128)(2,1)} %param.13, f32[5120]{0:T(1024)S(1)} %convert_element_type.75, f32[2,128]{1,0:T(2,128)S(1)} %add_rsqrt_fusion.1), kind=kLoop, calls=%fused_computation.24 | loop fusion | flops 7864320 | bytes 7885824 | tf_op jit(solution)/shard_map/convert_element_type | solution.py:32
  120.7 17.8 %fusion.4 = f32[2,128,3456]{2,1,0:T(8,128)} fusion(bf16[2,128,5120]{2,1,0:T(8,128)(2,1)S(1)} %fusion.26, bf16[5120,3456]{1,0:T(8,128)(2,1)} %param.23), kind=kOutput, calls=%fused_computation.4 | convolution fusion | flops 9059696640 | bytes 41549824 | tf_op jit(solution)/shard_map/bsd,df->bsf/dot_general | solution.py:63
  138.4 30.1 %fusion.14 = bf16[2,128,5120]{2,1,0:T(8,128)(2,1)} fusion(bf16[3456,5120]{1,0:T(8,128)(2,1)} %param.25, bf16[2,128,5120]{2,1,0:T(8,128)(2,1)S(1)} %fusion.26, bf16[5120,3456]{1,0:T(8,128)(2,1)} %param.24, f32[2,128,3456]{2,1,0:T(8,128)} %fusion.4), kind=kOutput, calls=%fused_computation.18 | convolution fusion | flops 18126012416 | bytes 79560704 | tf_op jit(solution)/shard_map/bsf,fd->bsd/dot_general | solution.py:66
  168.5 0.0 copy-start.9
  168.5 0.0 all-reduce.6.cloned.1.call-update
  168.5 1.1 copy.34
  169.6 2.2 copy.35
  171.8 0.0 copy-done.9
  171.8 53.0 %all-reduce.6.cloned.1.call-done = bf16[2,128,5120]{2,1,0:T(8,128)(2,1)} async-done(((bf16[2,128,5120]{2,1,0:T(8,128)(2,1)}), bf16[2,128,5120]{2,1,0:T(8,128)(2,1)}) %all-reduce.6.cloned.1.call-update) | async-done | bytes 2621456 | tf_op jit(solution)/shard_map/psum | solution.py:67
  224.8 0.0 copy-start
  224.8 2.5 %fusion.27 = f32[2,128]{1,0:T(2,128)S(1)} fusion(bf16[2,128,5120]{2,1,0:T(8,128)(2,1)} %all-reduce.6.cloned.1.call-done), kind=kLoop, calls=%fused_computation.25 | loop fusion | flops 3931904 | bytes 2622464 | tf_op jit(solution)/shard_map/reduce_sum | solution.py:27
  227.3 0.0 copy-done
  227.3 2.8 %fusion.30 = bf16[2,128,5120]{2,1,0:T(8,128)(2,1)} fusion(bf16[2,128,5120]{2,1,0:T(8,128)(2,1)S(1)} %copy-done, bf16[2,128,5120]{2,1,0:T(8,128)(2,1)S(1)} %fusion.26, f32[5120]{0:T(1024)S(1)} %convert_element_type.81, f32[2,128]{1,0:T(2,128)S(1)} %add_rsqrt_fusion), kind=kLoop, calls=%fused_computation.28 | loop fusion | flops 7864320 | bytes 7885824 | tf_op jit(solution)/shard_map/convert_element_type | solution.py:32
  (9 shorter events, 0.1 us)
Async XLA Ops:
  7.2 107.9 %all-reduce.4.cloned.1.call-start = ((), (), s32[]{:S(2)}) async-start(), calls=%async_computation | async-start | bytes 5242880 | tf_op jit(solution)/shard_map/psum | solution.py:61
  7.2 10.0 %copy-start.5 = (bf16[2,128,5120]{2,1,0:T(8,128)(2,1)S(1)}, bf16[2,128,5120]{2,1,0:T(8,128)(2,1)}, u32[]{:S(2)}) copy-start(bf16[2,128,5120]{2,1,0:T(8,128)(2,1)} %param.13) | copy-start | bytes 7864324
  7.3 10.0 %copy-start.12 = (bf16[5120,1280]{1,0:T(8,128)(2,1)S(1)}, bf16[5120,1280]{1,0:T(8,128)(2,1)}, u32[]{:S(2)}) copy-start(bf16[5120,1280]{1,0:T(8,128)(2,1)} %param.15) | copy-start | bytes 39321604
  17.3 4.6 %copy-start.10 = (bf16[1280]{0:T(1024)(128)(2,1)S(1)}, bf16[1280]{0:T(1024)(128)(2,1)}, u32[]{:S(2)}) copy-start(bf16[1280]{0:T(1024)(128)(2,1)} %param.20) | copy-start | bytes 7684
  30.7 1.9 copy-start.11
  31.1 1.8 copy-start.7
  34.2 2.9 %copy-start.13 = (s32[2]{0:T(128)S(1)}, s32[2]{0:T(128)}, u32[]{:S(2)}) copy-start(s32[2]{0:T(128)} %param.14) | copy-start | bytes 28
  35.9 2.2 copy-start.6
  45.9 1.7 copy-start.2
  45.9 1.7 copy-start.3
  47.6 1.1 copy-start.4
  58.7 0.7 copy-start.8
  58.8 166.1 %all-reduce.6.cloned.1.call-start = ((), (), s32[]{:S(2)}) async-start(), calls=%async_computation.1 | async-start | bytes 5242880 | tf_op jit(solution)/shard_map/psum | solution.py:67
  115.1 2.5 %copy-start.1 = (bf16[2,128,5120]{2,1,0:T(8,128)(2,1)S(1)}, bf16[2,128,5120]{2,1,0:T(8,128)(2,1)}, u32[]{:S(2)}) copy-start(bf16[2,128,5120]{2,1,0:T(8,128)(2,1)} %all-reduce.4.cloned.1.call-done) | copy-start | bytes 7864324
  168.5 3.3 %copy-start.9 = (bf16[5120]{0:T(1024)(128)(2,1)S(1)}, bf16[5120]{0:T(1024)(128)(2,1)}, u32[]{:S(2)}) copy-start(bf16[5120]{0:T(1024)(128)(2,1)} %param.22) | copy-start | bytes 30724
  224.8 2.5 %copy-start = (bf16[2,128,5120]{2,1,0:T(8,128)(2,1)S(1)}, bf16[2,128,5120]{2,1,0:T(8,128)(2,1)}, u32[]{:S(2)}) copy-start(bf16[2,128,5120]{2,1,0:T(8,128)(2,1)} %all-reduce.6.cloned.1.call-done) | copy-start | bytes 7864324
Sparse Core Ops, SparseCore 0:
  58.9 56.1 all-reduce.3
  168.7 56.1 all-reduce.5
where the time goes:
time: 237 us
  waiting for transfers between devices  109 us (46%)
  matrix products  79.7 us (34%)
  other arithmetic  16.9 us (7%)
  between operations  14.2 us (6%)
  local copies, waits for them, and re-layouts  8.66 us (4%)
  blocking collectives  8.61 us (4%)
    psum x1, waiting for transfers between devices, local_layer(): attn_proj = lax.psum(attn_part, 'tp')  55.6 us
    psum x1, waiting for transfers between devices, local_layer(): mlp_out = lax.psum(mlp_part, 'tp')  53 us
    dot_general x1, matrix products, local_layer(): jnp.einsum('bsf,fd->bsd', act_out, w_down, preferred_element_type=jnp.flo...  30.1 us
    dot_general x1, matrix products, local_layer(): jnp.einsum('bsd,df->bsf', hidden, w_gate, preferred_element_type=jnp.floa...  17.8 us
    dot_general x1, matrix products, local_layer(): jnp.einsum('bsd,dn->bsn', tokens, w_k, preferred_element_type=jnp.float32)  9.95 us
    dot_general x1, matrix products, local_layer(): jnp.einsum('bsn,nd->bsd', attn_out.reshape(prompts, seq_len, -1), w_o, pr...  9.69 us
    psum x1, blocking collectives, local_layer(): k_sumsq = lax.psum(jnp.sum(k_raw * k_raw, axis=-1, keepdims=True), 'tp')  8.61 us
    dot_general x1, matrix products, local_layer(): jnp.einsum('bsd,dn->bsn', tokens, w_v, preferred_element_type=jnp.float32)  6.68 us
  transfers between devices with their start and end apart: 2, of which 2 were waited for; matrix products, arithmetic and copies ran while one was open for 1% of the time, Pallas kernels for 0%

commit v1 on v0

v1 whole, which is shorter than its diff:
```python
import functools

import numpy as np
import jax
import jax.numpy as jnp
from jax import lax
from jax.experimental import pallas as pl
from jax.experimental.pallas import tpu as pltpu
from jax.sharding import PartitionSpec as P

HEAD_DIM = 128
ROPE_BASE = 500000.0
NORM_EPS = 1e-6
SLOTS = 13
F32 = jnp.float32
BF16 = jnp.bfloat16


def rope_tables(seq_len):
    half = HEAD_DIM // 2
    inv_freq = (ROPE_BASE ** (-2.0 * np.arange(half) / HEAD_DIM)).astype(np.float32)
    angles = np.arange(seq_len, dtype=np.float32)[:, None] * inv_freq[None, :]
    cos, sin = np.cos(angles), np.sin(angles)
    return (np.concatenate([cos, cos], -1).astype(np.float32), np.concatenate([-sin, sin], -1).astype(np.float32))


def layer_kernel(seq_ref, cos_ref, sin_ref, gq_ref, gk_ref, ga_ref, gm_ref,
                 x_hbm, wq, wk, wv, wo, wg, wu, wd,
                 y_hbm, kc_hbm, vc_hbm,
                 pool, x, qraw, kraw, kb, vb, o, act, ssq_acc, rsc, ssq_send, ssq_recv,
                 rs_send, rs_recv, xs_send, xs_recv, full,
                 wsem, xsem, csem, ysem, ssq_s, ssq_r, arsem):
    dp = lax.axis_index("dp")
    t = lax.axis_index("tp")
    core = lax.rem(t, 2)
    sib = t + 1 - 2 * core
    xpeer = lax.rem(t + 2, 4)
    diag = 3 - t
    width = 5120

    B_V, B_O, B_G, B_D, B_END = 10, 15, 20, 47, 67

    def half_col(step, per):
        return lax.rem(step, per) + per * lax.rem(step // per + 1 + core, 2)

    def cols(start, size):
        return pl.ds(pl.multiple_of(start, size), size)

    def issue(n, lo, hi):
        slot = lax.rem(n, SLOTS)
        sem = wsem.at[slot]

        def copy(src, dst):
            pltpu.make_async_copy(src, dst, sem).start()

        def do_qk():
            @pl.when(lax.rem(n, 2) == 0)
            def _():
                copy(wq.at[:, cols((n // 2) * 256, 256)], pool.at[slot])

            @pl.when(lax.rem(n, 2) == 1)
            def _():
                copy(wk.at[:, cols((n // 2) * 256, 256)], pool.at[slot])

        def do_v():
            copy(wv.at[:, cols((n - B_V) * 256, 256)], pool.at[slot])

        def do_o():
            for k in range(4):
                step = 2 * (n - B_O) + k // 2
                copy(wo.at[:, cols(half_col(step, 5) * 512 + (k % 2) * 256, 256)], pool.at[slot, pl.ds(k * 1280, 1280), :])

        def do_g():
            r = n - B_G

            @pl.when(jnp.logical_and(lax.rem(r, 2) == 0, r < 26))
            def _():
                copy(wg.at[:, cols((r // 2) * 256, 256)], pool.at[slot])

            @pl.when(lax.rem(r, 2) == 1)
            def _():
                copy(wu.at[:, cols((r // 2) * 256, 256)], pool.at[slot])

            @pl.when(r == 26)
            def _():
                copy(wg.at[:, pl.ds(3328, 128)], pool.at[slot, :, pl.ds(0, 128)])
                copy(wu.at[:, pl.ds(3328, 128)], pool.at[slot, :, pl.ds(128, 128)])

        def do_d():
            copy(wd.at[:, cols(half_col(n - B_D, 10) * 256, 256)], pool.at[slot, pl.ds(0, 3456), :])

        for start, end, fn in ((0, B_V, do_qk), (B_V, B_O, do_v), (B_O, B_G, do_o), (B_G, B_D, do_g), (B_D, B_END, do_d)):
            if hi < start or lo >= end:
                continue
            if lo >= start and hi < end:
                fn()
            else:
                pl.when(jnp.logical_and(n >= start, n < end))(fn)

    def wait_chunk(n, rows=5120):
        slot = lax.rem(n, SLOTS)
        src = wq if rows == 5120 else wd
        pltpu.make_async_copy(src.at[:, pl.ds(0, 256)], pool.at[slot, pl.ds(0, rows), :], wsem.at[slot]).wait()
        return slot

    def dot(a, b):
        return jnp.dot(a, b, preferred_element_type=F32)

    xcopy = pltpu.make_async_copy(x_hbm, x, xsem)
    xcopy.start()
    for n in range(SLOTS):
        issue(jnp.int32(n), n, n)

    barrier = pltpu.get_barrier_semaphore()
    for peer in (sib, xpeer, diag):
        pl.semaphore_signal(barrier, inc=1, device_id={"tp": peer}, device_id_type=pl.DeviceIdType.MESH)
    pl.semaphore_wait(barrier, 3)

    def remote(src, dst, ssem, rsem, peer):
        return pltpu.make_async_remote_copy(src_ref=src, dst_ref=dst, send_sem=ssem, recv_sem=rsem,
                                            device_id={"tp": peer}, device_id_type=pl.DeviceIdType.MESH)

    xcopy.wait()
    ssq_acc[...] = jnp.zeros_like(ssq_acc)

    def qk_step(i, carry):
        n = 2 * i
        s0 = wait_chunk(n)
        s1 = wait_chunk(n + 1)
        q = dot(x[...], pool[s0])
        k = dot(x[...], pool[s1])
        for b in range(2):
            for hh in range(2):
                qraw[b, 2 * i + hh] = q[b * 128:(b + 1) * 128, hh * 128:(hh + 1) * 128]
                kraw[b, 2 * i + hh] = k[b * 128:(b + 1) * 128, hh * 128:(hh + 1) * 128]
        ssq_acc[0] += q[:, :128] * q[:, :128] + q[:, 128:] * q[:, 128:]
        ssq_acc[1] += k[:, :128] * k[:, :128] + k[:, 128:] * k[:, 128:]
        issue(n + SLOTS, SLOTS, SLOTS + 8)
        issue(n + 1 + SLOTS, SLOTS + 1, SLOTS + 9)
        return carry

    lax.fori_loop(0, 5, qk_step, 0)

    for r in range(2):
        ssq_send[r:r + 1, :] = jnp.sum(jnp.transpose(ssq_acc[r]), axis=0, keepdims=True)
    ssq_send[2:8, :] = jnp.zeros((6, 256), F32)
    ssq_copies = [remote(ssq_send, ssq_recv.at[j], ssq_s.at[j], ssq_r.at[j], peer) for j, peer in enumerate((sib, xpeer, diag))]
    for c in ssq_copies:
        c.start()

    for group in ((10, 11), (12, 13), (14,)):
        slots = [wait_chunk(jnp.int32(n)) for n in group]
        vals = [dot(x[...], pool[s]).astype(BF16) for s in slots]
        for n, v in zip(group, vals):
            for b in range(2):
                for hh in range(2):
                    vb[b, 2 * (n - B_V) + hh] = v[b * 128:(b + 1) * 128, hh * 128:(hh + 1) * 128]
        for n in group:
            issue(jnp.int32(n + SLOTS), n + SLOTS, n + SLOTS)
    vcopy = pltpu.make_async_copy(vb, vc_hbm, csem.at[0])
    vcopy.start()

    for c in ssq_copies:
        c.wait()
    total = ssq_send[...] + ssq_recv[0] + ssq_recv[1] + ssq_recv[2]
    scale = lax.rsqrt(total * (1.0 / width) + NORM_EPS)
    for r in range(2):
        rsc[r] = jnp.transpose(jnp.broadcast_to(scale[r:r + 1, :], (128, 256)))

    row = lax.broadcasted_iota(jnp.int32, (128, 128), 0)
    col = lax.broadcasted_iota(jnp.int32, (128, 128), 1)

    def rope(v):
        return (v * cos_ref[...] + pltpu.roll(v, 64, 1) * sin_ref[...]).astype(BF16)

    for b in range(2):
        allowed = jnp.logical_and(col <= row, col < seq_ref[b])

        def attn_step(i, carry, b=b, allowed=allowed):
            for u in range(5):
                h = i * 5 + u
                hs = cols(h * 128, 128)
                q = rope(qraw[b, h] * rsc[0, b * 128:(b + 1) * 128, :] * gq_ref[:, hs])
                k = rope(kraw[b, h] * rsc[1, b * 128:(b + 1) * 128, :] * gk_ref[:, hs])
                kb[b, h] = k
                s = lax.dot_general(q, k, (((1,), (1,)), ((), ())), preferred_element_type=F32) * HEAD_DIM ** -0.5
                s = jnp.where(allowed, s, -1e30)
                e = jnp.exp(s - jnp.max(s, axis=-1, keepdims=True))
                p = (e / jnp.sum(e, axis=-1, keepdims=True)).astype(BF16)
                o[b * 128:(b + 1) * 128, hs] = dot(p, vb[b, h]).astype(BF16)
            return carry

        lax.fori_loop(0, 2, attn_step, 0)
    kcopy = pltpu.make_async_copy(kb, kc_hbm, csem.at[1])
    kcopy.start()

    def rs_copy(p, j):
        return remote(rs_send.at[p, j], rs_recv.at[p, j], arsem.at[p, 0, j], arsem.at[p, 1, j], sib)

    def xs_copy(p, j):
        return remote(xs_send.at[p, j], xs_recv.at[p, j], arsem.at[p, 2, j], arsem.at[p, 3, j], xpeer)

    def ag_copy(p, j, owner):
        blk = full.at[p, owner * 5 + j]
        return remote(blk, blk, arsem.at[p, 4, j], arsem.at[p, 5, j], sib)

    def reduce_columns(p, partial):
        def sib_step(j, carry):
            rs_send[p, j] = partial(j).astype(BF16)
            rs_copy(p, j).start()
            return carry

        lax.fori_loop(0, 5, sib_step, 0)

        def own_step(j, carry):
            val = partial(j + 5)
            rs_copy(p, j).wait()
            xs_send[p, j] = (val + rs_recv[p, j].astype(F32)).astype(BF16)
            xs_copy(p, j).start()
            return carry

        lax.fori_loop(0, 5, own_step, 0)

        def gather_step(j, carry):
            xs_copy(p, j).wait()
            full[p, core * 5 + j] = (xs_send[p, j].astype(F32) + xs_recv[p, j].astype(F32)).astype(BF16)
            ag_copy(p, j, core).start()
            return carry

        lax.fori_loop(0, 5, gather_step, 0)

        def arrive_step(j, carry):
            ag_copy(p, j, core).wait_send()
            ag_copy(p, j, 1 - core).wait_recv()
            return carry

        lax.fori_loop(0, 5, arrive_step, 0)

    def post_norm(p, gain):
        def sq(c, acc):
            v = full[p, c].astype(F32)
            return acc + v[:, :128] * v[:, :128] + v[:, 128:256] * v[:, 128:256] + v[:, 256:384] * v[:, 256:384] + v[:, 384:] * v[:, 384:]

        acc = lax.fori_loop(0, 10, sq, jnp.zeros((256, 128), F32))
        rs = lax.rsqrt(jnp.sum(acc, axis=-1, keepdims=True) * (1.0 / width) + NORM_EPS)

        def apply(c, carry):
            cs = cols(c * 512, 512)
            x[:, cs] = (x[:, cs].astype(F32) + full[p, c].astype(F32) * rs * gain[:, cs]).astype(BF16)
            return carry

        lax.fori_loop(0, 10, apply, 0)

    def o_partial(step):
        n = B_O + step // 2
        slot = lax.rem(n, SLOTS)

        @pl.when(lax.rem(step, 2) == 0)
        def _():
            wait_chunk(n)

        base = lax.rem(step, 2) * 2560
        parts = [dot(o[...], pool[slot, pl.ds(pl.multiple_of(base + k * 1280, 1280), 1280), :]) for k in range(2)]

        @pl.when(lax.rem(step, 2) == 1)
        def _():
            issue(n + SLOTS, B_O + SLOTS, B_O + SLOTS + 4)

        return jnp.concatenate(parts, axis=1)

    reduce_columns(0, o_partial)
    post_norm(0, ga_ref)

    def gu_step(i, carry):
        n = B_G + 2 * i
        s0 = wait_chunk(n)
        s1 = wait_chunk(n + 1)
        g = dot(x[...], pool[s0])
        u = dot(x[...], pool[s1])
        act[:, cols(i * 256, 256)] = (g * jax.nn.sigmoid(g) * u).astype(BF16)
        issue(n + SLOTS, B_G + SLOTS, B_D + SLOTS - 2)
        issue(n + 1 + SLOTS, B_G + 1 + SLOTS, B_D + SLOTS - 2)
        return carry

    lax.fori_loop(0, 13, gu_step, 0)
    s0 = wait_chunk(jnp.int32(B_D - 1))
    gu = dot(x[...], pool[s0])
    act[:, 3328:3456] = (gu[:, :128] * jax.nn.sigmoid(gu[:, :128]) * gu[:, 128:]).astype(BF16)
    issue(jnp.int32(B_D - 1 + SLOTS), B_D - 1 + SLOTS, B_D - 1 + SLOTS)

    def d_partial(step):
        n = B_D + 2 * step
        s0 = wait_chunk(n, 3456)
        s1 = wait_chunk(n + 1, 3456)
        parts = [dot(act[...], pool[s, pl.ds(0, 3456), :]) for s in (s0, s1)]
        for q in (n, n + 1):
            @pl.when(q + SLOTS < B_END)
            def _(q=q):
                issue(q + SLOTS, B_D + SLOTS, B_END - 1)
        return jnp.concatenate(parts, axis=1)

    reduce_columns(1, d_partial)
    post_norm(1, gm_ref)
    ycopy = pltpu.make_async_copy(x, y_hbm, ysem)
    ycopy.start()
    vcopy.wait()
    kcopy.wait()
    ycopy.wait()


def solution(mesh):
    def local_layer(tokens, seq_lens, w_q, w_k, w_v, w_o, g_q, g_k, g_attn, g_mlp, w_gate, w_up, w_down):
        cos_tab, sin_tab = rope_tables(128)
        vmem = pl.BlockSpec(memory_space=pltpu.VMEM)
        hbm = pl.BlockSpec(memory_space=pl.ANY)
        gain = lambda g: g.astype(F32).reshape(1, -1)
        dma = pltpu.SemaphoreType.DMA
        y, kc, vc = pl.pallas_call(
            layer_kernel,
            out_shape=(jax.ShapeDtypeStruct((256, 5120), BF16), jax.ShapeDtypeStruct((2, 10, 128, 128), BF16), jax.ShapeDtypeStruct((2, 10, 128, 128), BF16)),
            in_specs=[pl.BlockSpec(memory_space=pltpu.SMEM)] + [vmem] * 6 + [hbm] * 8,
            out_specs=(hbm, hbm, hbm),
            scratch_shapes=[
                pltpu.VMEM((SLOTS, 5120, 256), BF16),
                pltpu.VMEM((256, 5120), BF16),
                pltpu.VMEM((2, 10, 128, 128), F32),
                pltpu.VMEM((2, 10, 128, 128), F32),
                pltpu.VMEM((2, 10, 128, 128), BF16),
                pltpu.VMEM((2, 10, 128, 128), BF16),
                pltpu.VMEM((256, 1280), BF16),
                pltpu.VMEM((256, 3456), BF16),
                pltpu.VMEM((2, 256, 128), F32),
                pltpu.VMEM((2, 256, 128), F32),
                pltpu.VMEM((8, 256), F32),
                pltpu.VMEM((3, 8, 256), F32),
                pltpu.VMEM((2, 5, 256, 512), BF16),
                pltpu.VMEM((2, 5, 256, 512), BF16),
                pltpu.VMEM((2, 5, 256, 512), BF16),
                pltpu.VMEM((2, 5, 256, 512), BF16),
                pltpu.VMEM((2, 10, 256, 512), BF16),
                dma((SLOTS,)), dma, dma((2,)), dma, dma((3,)), dma((3,)), dma((2, 6, 5)),
            ],
            compiler_params=pltpu.CompilerParams(collective_id=0, has_side_effects=True, vmem_limit_bytes=67043328),
        )(seq_lens, jnp.asarray(cos_tab), jnp.asarray(sin_tab), gain(g_q), gain(g_k), gain(g_attn), gain(g_mlp),
          tokens.reshape(256, 5120), w_q, w_k, w_v, w_o, w_gate, w_up, w_down)
        return y.reshape(2, 128, 5120), kc, vc

    return jax.shard_map(local_layer, mesh=mesh, in_specs=(P('dp', None, None), P('dp'), P(None, 'tp'), P(None, 'tp'), P(None, 'tp'), P('tp', None), P('tp'), P('tp'), P(), P(), P(None, 'tp'), P(None, 'tp'), P('tp', None)), out_specs=(P('dp', None, None), P('dp', 'tp', None, None), P('dp', 'tp', None, None)), check_vma=False)
```

time: 237 us -> 146 us (0.62)
  Pallas kernels: 0 us -> 133 us
  waiting for transfers between devices: 109 us -> 0 us
  matrix products: 79.7 us -> 0 us
  other arithmetic: 16.9 us -> 2.62 us
  between operations: 14.2 us -> 0.64 us
  blocking collectives: 8.61 us -> 0 us
    pallas_call x0 -> x1, Pallas kernels: none -> 133 us  [local_layer(): pl.pallas_call(layer_kernel, out_shape=(jax.ShapeDtypeStruct((256, 5120),...]
    psum x2 -> x0, waiting for transfers between devices: 109 us -> none  [the longest x1 55.6 us: local_layer(): attn_proj = lax.psum(attn_part, 'tp')]
    dot_general x8 -> x0, matrix products: 79.7 us -> none  [the longest x1 30.1 us: local_layer(): jnp.einsum('bsf,fd->bsd', act_out, w_down, preferred_element_type=jnp.flo...]
    psum x1 -> x0, blocking collectives: 8.61 us -> none  [local_layer(): k_sumsq = lax.psum(jnp.sum(k_raw * k_raw, axis=-1, keepdims=True), 'tp')]
    convert_element_type x6 -> x0, other arithmetic: 5.88 us -> none  [the longest x2 5.86 us: post_norm(): (base.astype(jnp.float32) + branch32 * rms_scale(branch32) * gain.astype(...]
    reduce_sum x3 -> x0, other arithmetic: 5.17 us -> none  [the longest x2 4.98 us: rms_scale(): return lax.rsqrt(jnp.mean(vals * vals, axis=-1, keepdims=True) + NORM_EPS)]
    reshape x0 -> x2, other arithmetic: none -> 2.62 us  [local_layer(): gain = lambda g: g.astype(F32).reshape(1, -1)]
    reshape x0 -> x2, local copies, waits for them, and re-layouts: none -> 2.56 us  [local_layer(): gain = lambda g: g.astype(F32).reshape(1, -1)]
  transfers between devices with their start and end apart: 2 -> 0, of which waited for: 2 -> 0; matrix products, arithmetic and copies ran while one was open for 1% -> 0% of each run, Pallas kernels for 0% -> 0%
where the time goes in v1:
time: 146 us
  Pallas kernels  133 us (91%)
  local copies, waits for them, and re-layouts  9.93 us (7%)
  other arithmetic  2.62 us (2%)
    pallas_call x1, Pallas kernels, local_layer(): pl.pallas_call(layer_kernel, out_shape=(jax.ShapeDtypeStruct((256, 5120),...  133 us
    unnamed x3, local copies, waits for them, and re-layouts  7.37 us

profile of v1, /device:TPU:0, one launch (start us, length us, event | category | flops | bytes accessed | tf_op | source)
XLA Modules:
  0.0 145.9 jit_solution(15820782544057365892)
XLA Ops:
  0.6 1.3 reshape.43.gq_ref
  1.9 1.3 reshape.45.gk_ref
  3.2 1.3 reshape.46
  4.5 1.3 reshape.48
  5.8 132.7 %shard_map.166 = (bf16[256,5120]{1,0:T(8,128)(2,1)}, bf16[2,10,128,128]{3,2,1,0:T(8,128)(2,1)}, bf16[2,10,128,128]{3,2,1,0:T(8,128)(2,1)}) custom-call(s32[2]{0:T(128)} %seq_ref.1, f32[128,128]{1,0:T(8,128)} %constant.4.clone.cos_ref, f32[128,128]{1,0:T(8,128)} %constant.5.clone.sin_ref, f32[1,1280]{1,0:T(1,128)} %reshape.43.gq_ref, ...), custom_call_target="tpu_custom_call" | custom-call | tf_op jit(solution)/shard_map/pallas_call | solution.py:318
  138.5 3.4 %copy.21 = bf16[2,128,5120]{2,1,0:T(8,128)(2,1)} copy(bf16[2,128,5120]{2,1,0:T(8,128)(2,1)} %bitcast.4) | data formatting | bytes 5242880
  141.9 2.0 %copy.22 = bf16[2,10,128,128]{3,2,1,0:T(8,128)(2,1)} copy(bf16[2,10,128,128]{3,2,1,0:T(8,128)(2,1)} %get-tuple-element.13) | data formatting | bytes 1310720
  143.9 2.0 %copy.23 = bf16[2,10,128,128]{3,2,1,0:T(8,128)(2,1)} copy(bf16[2,10,128,128]{3,2,1,0:T(8,128)(2,1)} %get-tuple-element.14) | data formatting | bytes 1310720

commit v2 on v1

--- a/solution.py
+++ b/solution.py
@@ -24,12 +24,13 @@
     return (np.concatenate([cos, cos], -1).astype(np.float32), np.concatenate([-sin, sin], -1).astype(np.float32))
 
 
-def layer_kernel(seq_ref, cos_ref, sin_ref, gq_ref, gk_ref, ga_ref, gm_ref,
+def layer_kernel(seq_ref, cos_hbm, sin_hbm, gq_hbm, gk_hbm, ga_hbm,
                  x_hbm, wq, wk, wv, wo, wg, wu, wd,
-                 y_hbm, kc_hbm, vc_hbm,
+                 h_hbm, m_hbm, rs_hbm, kc_hbm, vc_hbm,
                  pool, x, qraw, kraw, kb, vb, o, act, ssq_acc, rsc, ssq_send, ssq_recv,
                  rs_send, rs_recv, xs_send, xs_recv, full,
-                 wsem, xsem, csem, ysem, ssq_s, ssq_r, arsem):
+                 cos_ref, sin_ref, gq16, gk16, ga16, gq_ref, gk_ref, ga_ref, sq_acc, rs_out,
+                 wsem, xsem, csem, ysem, ssq_s, ssq_r, arsem, tsem):
     dp = lax.axis_index("dp")
     t = lax.axis_index("tp")
     core = lax.rem(t, 2)
@@ -110,16 +111,25 @@
     xcopy.start()
     for n in range(SLOTS):
         issue(jnp.int32(n), n, n)
+    small = [pltpu.make_async_copy(src, dst, tsem.at[i]) for i, (src, dst) in enumerate(
+        ((cos_hbm, cos_ref), (sin_hbm, sin_ref), (gq_hbm, gq16), (gk_hbm, gk16), (ga_hbm, ga16)))]
+    for c in small:
+        c.start()
 
     barrier = pltpu.get_barrier_semaphore()
     for peer in (sib, xpeer, diag):
         pl.semaphore_signal(barrier, inc=1, device_id={"tp": peer}, device_id_type=pl.DeviceIdType.MESH)
-    pl.semaphore_wait(barrier, 3)
+    with jax.named_scope("barrier"):
+        pl.semaphore_wait(barrier, 3)
 
     def remote(src, dst, ssem, rsem, peer):
         return pltpu.make_async_remote_copy(src_ref=src, dst_ref=dst, send_sem=ssem, recv_sem=rsem,
                                             device_id={"tp": peer}, device_id_type=pl.DeviceIdType.MESH)
 
+    for c in small:
+        c.wait()
+    for src, dst in ((gq16, gq_ref), (gk16, gk_ref), (ga16, ga_ref)):
+        dst[...] = src[...].astype(F32)
     xcopy.wait()
     ssq_acc[...] = jnp.zeros_like(ssq_acc)
 
@@ -139,7 +149,8 @@
         issue(n + 1 + SLOTS, SLOTS + 1, SLOTS + 9)
         return carry
 
-    lax.fori_loop(0, 5, qk_step, 0)
+    with jax.named_scope("qk"):
+        lax.fori_loop(0, 5, qk_step, 0)
 
     for r in range(2):
         ssq_send[r:r + 1, :] = jnp.sum(jnp.transpose(ssq_acc[r]), axis=0, keepdims=True)
@@ -160,8 +171,9 @@
     vcopy = pltpu.make_async_copy(vb, vc_hbm, csem.at[0])
     vcopy.start()
 
-    for c in ssq_copies:
-        c.wait()
+    with jax.named_scope("ssqwait"):
+        for c in ssq_copies:
+            c.wait()
     total = ssq_send[...] + ssq_recv[0] + ssq_recv[1] + ssq_recv[2]
     scale = lax.rsqrt(total * (1.0 / width) + NORM_EPS)
     for r in range(2):
@@ -180,8 +192,8 @@
             for u in range(5):
                 h = i * 5 + u
                 hs = cols(h * 128, 128)
-                q = rope(qraw[b, h] * rsc[0, b * 128:(b + 1) * 128, :] * gq_ref[:, hs])
-                k = rope(kraw[b, h] * rsc[1, b * 128:(b + 1) * 128, :] * gk_ref[:, hs])
+                q = rope(qraw[b, h] * rsc[0, b * 128:(b + 1) * 128, :] * gq_ref[pl.ds(h, 1), :])
+                k = rope(kraw[b, h] * rsc[1, b * 128:(b + 1) * 128, :] * gk_ref[pl.ds(h, 1), :])
                 kb[b, h] = k
                 s = lax.dot_general(q, k, (((1,), (1,)), ((), ())), preferred_element_type=F32) * HEAD_DIM ** -0.5
                 s = jnp.where(allowed, s, -1e30)
@@ -190,7 +202,8 @@
                 o[b * 128:(b + 1) * 128, hs] = dot(p, vb[b, h]).astype(BF16)
             return carry
 
-        lax.fori_loop(0, 2, attn_step, 0)
+        with jax.named_scope("attn"):
+            lax.fori_loop(0, 2, attn_step, 0)
     kcopy = pltpu.make_async_copy(kb, kc_hbm, csem.at[1])
     kcopy.start()
 
@@ -210,7 +223,8 @@
             rs_copy(p, j).start()
             return carry
 
-        lax.fori_loop(0, 5, sib_step, 0)
+        with jax.named_scope(f"sib{p}"):
+            lax.fori_loop(0, 5, sib_step, 0)
 
         def own_step(j, carry):
             val = partial(j + 5)
@@ -219,34 +233,43 @@
             xs_copy(p, j).start()
             return carry
 
-        lax.fori_loop(0, 5, own_step, 0)
+        with jax.named_scope(f"own{p}"):
+            lax.fori_loop(0, 5, own_step, 0)
+
+        def squares(c):
+            v = full[p, c].astype(F32)
+            return v[:, :128] * v[:, :128] + v[:, 128:256] * v[:, 128:256] + v[:, 256:384] * v[:, 256:384] + v[:, 384:] * v[:, 384:]
+
+        sq_acc[...] = jnp.zeros_like(sq_acc)
 
         def gather_step(j, carry):
-            xs_copy(p, j).wait()
+            with jax.named_scope(f"xwait{p}"):
+                xs_copy(p, j).wait()
             full[p, core * 5 + j] = (xs_send[p, j].astype(F32) + xs_recv[p, j].astype(F32)).astype(BF16)
             ag_copy(p, j, core).start()
-            return carry
-
-        lax.fori_loop(0, 5, gather_step, 0)
+            sq_acc[0] += squares(core * 5 + j)
+            return carry
+
+        with jax.named_scope(f"gather{p}"):
+            lax.fori_loop(0, 5, gather_step, 0)
 
         def arrive_step(j, carry):
             ag_copy(p, j, core).wait_send()
             ag_copy(p, j, 1 - core).wait_recv()
-            return carry
-
-        lax.fori_loop(0, 5, arrive_step, 0)
-
-    def post_norm(p, gain):
-        def sq(c, acc):
-            v = full[p, c].astype(F32)
-            return acc + v[:, :128] * v[:, :128] + v[:, 128:256] * v[:, 128:256] + v[:, 256:384] * v[:, 256:384] + v[:, 384:] * v[:, 384:]
-
-        acc = lax.fori_loop(0, 10, sq, jnp.zeros((256, 128), F32))
-        rs = lax.rsqrt(jnp.sum(acc, axis=-1, keepdims=True) * (1.0 / width) + NORM_EPS)
+            sq_acc[1] += squares((1 - core) * 5 + j)
+            return carry
+
+        with jax.named_scope(f"arrive{p}"):
+            lax.fori_loop(0, 5, arrive_step, 0)
+        return lax.rsqrt(jnp.sum(sq_acc[0] + sq_acc[1], axis=-1, keepdims=True) * (1.0 / width) + NORM_EPS)
+
+    def post_norm(rs, gain):
+        rsb = jnp.broadcast_to(rs, (256, 128))
 
         def apply(c, carry):
-            cs = cols(c * 512, 512)
-            x[:, cs] = (x[:, cs].astype(F32) + full[p, c].astype(F32) * rs * gain[:, cs]).astype(BF16)
+            for w in range(4):
+                cs = cols(c * 512 + w * 128, 128)
+                x[:, cs] = (x[:, cs].astype(F32) + full[0, c, :, pl.ds(w * 128, 128)].astype(F32) * rsb * gain[pl.ds(c * 4 + w, 1), :]).astype(BF16)
             return carry
 
         lax.fori_loop(0, 10, apply, 0)
@@ -268,8 +291,12 @@
 
         return jnp.concatenate(parts, axis=1)
 
-    reduce_columns(0, o_partial)
-    post_norm(0, ga_ref)
+    with jax.named_scope("ar1"):
+        rs = reduce_columns(0, o_partial)
+    with jax.named_scope("norm1"):
+        post_norm(rs, ga_ref)
+    hcopy = pltpu.make_async_copy(x, h_hbm, ysem.at[0])
+    hcopy.start()
 
     def gu_step(i, carry):
         n = B_G + 2 * i
@@ -282,7 +309,8 @@
         issue(n + 1 + SLOTS, B_G + 1 + SLOTS, B_D + SLOTS - 2)
         return carry
 
-    lax.fori_loop(0, 13, gu_step, 0)
+    with jax.named_scope("gu"):
+        lax.fori_loop(0, 13, gu_step, 0)
     s0 = wait_chunk(jnp.int32(B_D - 1))
     gu = dot(x[...], pool[s0])
     act[:, 3328:3456] = (gu[:, :128] * jax.nn.sigmoid(gu[:, :128]) * gu[:, 128:]).astype(BF16)
@@ -299,27 +327,65 @@
                 issue(q + SLOTS, B_D + SLOTS, B_END - 1)
         return jnp.concatenate(parts, axis=1)
 
-    reduce_columns(1, d_partial)
-    post_norm(1, gm_ref)
-    ycopy = pltpu.make_async_copy(x, y_hbm, ysem)
-    ycopy.start()
-    vcopy.wait()
-    kcopy.wait()
-    ycopy.wait()
+    with jax.named_scope("ar2"):
+        rs = reduce_columns(1, d_partial)
+    with jax.named_scope("tail"):
+        rs_out[...] = jnp.broadcast_to(rs, (256, 128))
+        mcopy = pltpu.make_async_copy(full.at[1], m_hbm, ysem.at[1])
+        mcopy.start()
+        rcopy = pltpu.make_async_copy(rs_out, rs_hbm, ysem.at[2])
+        rcopy.start()
+        for c in (vcopy, kcopy, hcopy, mcopy, rcopy):
+            c.wait()
+
+
+def finish_kernel(rs_hbm, gm_hbm, h_hbm, m_hbm, k_in, v_in, y_hbm, k_out, v_out, rs, gm, h, m, kb, vb, isem, msem, hsem, osem, ysem):
+    copies = [pltpu.make_async_copy(src, dst, isem.at[i]) for i, (src, dst) in enumerate(((rs_hbm, rs), (gm_hbm, gm), (k_in, kb), (v_in, vb)))]
+    for c in copies[:2]:
+        c.start()
+
+    def halves(c):
+        return [pltpu.make_async_copy(m_hbm.at[c], m.at[c], msem.at[c]), pltpu.make_async_copy(h_hbm.at[:, pl.ds(c * 512, 512)], h.at[:, pl.ds(c * 512, 512)], hsem.at[c])]
+
+    for c in range(10):
+        for d in halves(c):
+            d.start()
+    for c in copies[2:]:
+        c.start()
+    copies[0].wait()
+    copies[1].wait()
+    out = []
+    for c in range(10):
+        for d in halves(c):
+            d.wait()
+        for w in range(4):
+            cs = pl.ds(c * 512 + w * 128, 128)
+            g = gm[c * 4 + w:c * 4 + w + 1, :].astype(F32)
+            h[:, cs] = (h[:, cs].astype(F32) + m[c, :, pl.ds(w * 128, 128)].astype(F32) * rs[...] * g).astype(BF16)
+        cs = pl.ds(c * 512, 512)
+        out.append(pltpu.make_async_copy(h.at[:, cs], y_hbm.at[:, cs], ysem.at[c]))
+        out[-1].start()
+    for i, (src, dst) in enumerate(((kb, k_out), (vb, v_out))):
+        copies[2 + i].wait()
+        out.append(pltpu.make_async_copy(src, dst, osem.at[i]))
+        out[-1].start()
+    for d in out:
+        d.wait()
 
 
 def solution(mesh):
     def local_layer(tokens, seq_lens, w_q, w_k, w_v, w_o, g_q, g_k, g_attn, g_mlp, w_gate, w_up, w_down):
         cos_tab, sin_tab = rope_tables(128)
-        vmem = pl.BlockSpec(memory_space=pltpu.VMEM)
         hbm = pl.BlockSpec(memory_space=pl.ANY)
-        gain = lambda g: g.astype(F32).reshape(1, -1)
+        gain = lambda g: g.reshape(-1, 128)
         dma = pltpu.SemaphoreType.DMA
-        y, kc, vc = pl.pallas_call(
+        cache = jax.ShapeDtypeStruct((2, 10, 128, 128), BF16)
+        hidden = jax.ShapeDtypeStruct((256, 5120), BF16)
+        h, m, rs, kc, vc = pl.pallas_call(
             layer_kernel,
-            out_shape=(jax.ShapeDtypeStruct((256, 5120), BF16), jax.ShapeDtypeStruct((2, 10, 128, 128), BF16), jax.ShapeDtypeStruct((2, 10, 128, 128), BF16)),
-            in_specs=[pl.BlockSpec(memory_space=pltpu.SMEM)] + [vmem] * 6 + [hbm] * 8,
-            out_specs=(hbm, hbm, hbm),
+            out_shape=(hidden, jax.ShapeDtypeStruct((10, 256, 512), BF16), jax.ShapeDtypeStruct((256, 128), F32), cache, cache),
+            in_specs=[pl.BlockSpec(memory_space=pltpu.SMEM)] + [hbm] * 13,
+            out_specs=(hbm,) * 5,
             scratch_shapes=[
                 pltpu.VMEM((SLOTS, 5120, 256), BF16),
                 pltpu.VMEM((256, 5120), BF16),
@@ -338,11 +404,37 @@
                 pltpu.VMEM((2, 5, 256, 512), BF16),
                 pltpu.VMEM((2, 5, 256, 512), BF16),
                 pltpu.VMEM((2, 10, 256, 512), BF16),
-                dma((SLOTS,)), dma, dma((2,)), dma, dma((3,)), dma((3,)), dma((2, 6, 5)),
+                pltpu.VMEM((128, 128), F32),
+                pltpu.VMEM((128, 128), F32),
+                pltpu.VMEM((10, 128), BF16),
+                pltpu.VMEM((10, 128), BF16),
+                pltpu.VMEM((40, 128), BF16),
+                pltpu.VMEM((10, 128), F32),
+                pltpu.VMEM((10, 128), F32),
+                pltpu.VMEM((40, 128), F32),
+                pltpu.VMEM((2, 256, 128), F32),
+                pltpu.VMEM((256, 128), F32),
+                dma((SLOTS,)), dma, dma((2,)), dma((3,)), dma((3,)), dma((3,)), dma((2, 6, 5)), dma((6,)),
             ],
             compiler_params=pltpu.CompilerParams(collective_id=0, has_side_effects=True, vmem_limit_bytes=67043328),
-        )(seq_lens, jnp.asarray(cos_tab), jnp.asarray(sin_tab), gain(g_q), gain(g_k), gain(g_attn), gain(g_mlp),
+        )(seq_lens, jnp.asarray(cos_tab), jnp.asarray(sin_tab), gain(g_q), gain(g_k), gain(g_attn),
           tokens.reshape(256, 5120), w_q, w_k, w_v, w_o, w_gate, w_up, w_down)
+        y, kc, vc = pl.pallas_call(
+            finish_kernel,
+            out_shape=(hidden, cache, cache),
+            in_specs=[hbm] * 6,
+            out_specs=(hbm,) * 3,
+            scratch_shapes=[
+                pltpu.VMEM((256, 128), F32),
+                pltpu.VMEM((40, 128), BF16),
+                pltpu.VMEM((256, 5120), BF16),
+                pltpu.VMEM((10, 256, 512), BF16),
+                pltpu.VMEM((2, 10, 128, 128), BF16),
+                pltpu.VMEM((2, 10, 128, 128), BF16),
+                dma((4,)), dma((10,)), dma((10,)), dma((2,)), dma((10,)),
+            ],
+            compiler_params=pltpu.CompilerParams(vmem_limit_bytes=60000000),
+        )(rs, gain(g_mlp), h, m, kc, vc)
         return y.reshape(2, 128, 5120), kc, vc
 
     return jax.shard_map(local_layer, mesh=mesh, in_specs=(P('dp', None, None), P('dp'), P(None, 'tp'), P(None, 'tp'), P(None, 'tp'), P('tp', None), P('tp'), P('tp'), P(), P(), P(None, 'tp'), P(None, 'tp'), P('tp', None)), out_specs=(P('dp', None, None), P('dp', 'tp', None, None), P('dp', 'tp', None, None)), check_vma=False)

time: 146 us -> 137 us (0.938)
  local copies, waits for them, and re-layouts: 9.93 us -> 0 us
  Pallas kernels: 133 us -> 136 us
  other arithmetic: 2.62 us -> 0 us
    unnamed x3 -> x0, local copies, waits for them, and re-layouts: 7.37 us -> none
    pallas_call x1 -> x2, Pallas kernels: 133 us -> 136 us  [the longest x1 132 us: local_layer(): pl.pallas_call(layer_kernel, out_shape=(hidden, jax.ShapeDtypeStruct((10,...]
    reshape x2 -> x0, other arithmetic: 2.62 us -> none  [local_layer(): gain = lambda g: g.astype(F32).reshape(1, -1)]
    reshape x2 -> x0, local copies, waits for them, and re-layouts: 2.56 us -> none  [local_layer(): gain = lambda g: g.astype(F32).reshape(1, -1)]
where the time goes in v2:
time: 137 us
  Pallas kernels  136 us (99%)
    pallas_call x1, Pallas kernels, local_layer(): pl.pallas_call(layer_kernel, out_shape=(hidden, jax.ShapeDtypeStruct((10,...  132 us
    pallas_call x1, Pallas kernels, local_layer(): pl.pallas_call(finish_kernel, out_shape=(hidden, cache, cache), in_specs=...  4.46 us

profile of v2, /device:TPU:0, one launch (start us, length us, event | category | flops | bytes accessed | tf_op | source)
XLA Modules:
  0.0 136.7 jit_solution(2260766546323324766)
XLA Ops:
  0.6 131.6 %shard_map.166 = (bf16[256,5120]{1,0:T(8,128)(2,1)}, bf16[10,256,512]{2,1,0:T(8,128)(2,1)}, f32[256,128]{1,0:T(8,128)}, bf16[2,10,128,128]{3,2,1,0:T(8,128)(2,1)}, bf16[2,10,128,128]{3,2,1,0:T(8,128)(2,1)}) custom-call(s32[2]{0:T(128)} %seq_ref.1, f32[128,128]{1,0:T(8,128)} %constant.4.clone.cos_hbm, f32[128,128]{1,0:T(8,128)} %constant.5.clone.sin_hbm, ...), custom_call_target="tpu_custom_call" | custom-call | tf_op jit(solution)/shard_map/pallas_call | solution.py:384
  132.3 4.5 %shard_map.167 = (bf16[256,5120]{1,0:T(8,128)(2,1)}, bf16[2,10,128,128]{3,2,1,0:T(8,128)(2,1)}, bf16[2,10,128,128]{3,2,1,0:T(8,128)(2,1)}) custom-call(f32[256,128]{1,0:T(8,128)} %get-tuple-element.11.rs_hbm, bf16[40,128]{1,0:T(8,128)(2,1)} %bitcast.8, bf16[256,5120]{1,0:T(8,128)(2,1)} %get-tuple-element.12.h_hbm, ...), custom_call_target="tpu_custom_call" | custom-call | tf_op jit(solution)/shard_map/pallas_call | solution.py:422

commit v3 on v0

v3 whole, which is shorter than its diff:
```python
import jax
import jax.numpy as jnp
import numpy as np
from jax import lax
from jax.experimental import pallas as pl
from jax.experimental.pallas import tpu as pltpu
from jax.sharding import PartitionSpec as P

HEAD_DIM = 128
ROPE_BASE = 500000.0
NORM_EPS = 1e-6
F32 = jnp.float32
BF16 = jnp.bfloat16

WIDTH = 5120
RING = 8
KEEP = 8
N_V, N_QKV = 10, 15
N_G = 27
N_RG = N_G - KEEP
N_MLP = N_RG + 20


def rope_tables(seq_len):
    half = HEAD_DIM // 2
    inv_freq = (ROPE_BASE ** (-2.0 * np.arange(half) / HEAD_DIM)).astype(np.float32)
    angles = np.arange(seq_len, dtype=np.float32)[:, None] * inv_freq[None, :]
    cos, sin = np.cos(angles), np.sin(angles)
    return (np.concatenate([cos, cos], -1).astype(np.float32), np.concatenate([-sin, sin], -1).astype(np.float32))


def cols(start, size):
    return pl.ds(pl.multiple_of(start, size), size)


def dot(a, b):
    return jnp.dot(a, b, preferred_element_type=F32)


def layer_kernel(seq_ref, cos_hbm, sin_hbm, gq_hbm, gk_hbm, ga_hbm,
                 x_hbm, wq, wk, wv, wo, wg, wu, wd,
                 h_hbm, m_hbm, rs_hbm, kc_hbm, vc_hbm,
                 pool, x, qraw, kraw, kb, vb, qb, o, act, own32, ssq_acc, rsc, ssq_send, ssq_recv,
                 rs_send, rs_recv, xs_send, xs_recv, full, sq_acc, rs_out,
                 cos_ref, sin_ref, gq16, gk16, ga16, gq_ref, gk_ref, ga_ref,
                 wsem, xsem, csem, ysem, ssq_s, ssq_r, arsem, tsem):
    t = lax.axis_index("tp")
    core = lax.rem(t, 2)
    sib = t + 1 - 2 * core
    xpeer = lax.rem(t + 2, 4)
    diag = 3 - t

    def load(src, dst, slot):
        pltpu.make_async_copy(src, dst, wsem.at[slot]).start()

    def load_qk(n):
        slot = lax.rem(n, RING)

        @pl.when(lax.rem(n, 2) == 0)
        def _():
            load(wq.at[:, cols((n // 2) * 256, 256)], pool.at[slot], slot)

        @pl.when(lax.rem(n, 2) == 1)
        def _():
            load(wk.at[:, cols((n // 2) * 256, 256)], pool.at[slot], slot)

    def load_v(n):
        slot = lax.rem(n, RING)
        load(wv.at[:, cols((n - N_V) * 256, 256)], pool.at[slot], slot)

    def load_o(j):
        slot = RING + j
        for k in range(4):
            half = core if k // 2 else 1 - core
            load(wo.at[:, cols(half * 2560 + j * 512 + (k % 2) * 256, 256)], pool.at[slot, pl.ds(k * 1280, 1280), :], slot)

    def load_g(k, slot):
        @pl.when(jnp.logical_and(lax.rem(k, 2) == 0, k < N_G - 1))
        def _():
            load(wg.at[:, cols((k // 2) * 256, 256)], pool.at[slot], slot)

        @pl.when(lax.rem(k, 2) == 1)
        def _():
            load(wu.at[:, cols((k // 2) * 256, 256)], pool.at[slot], slot)

        @pl.when(k == N_G - 1)
        def _():
            load(wg.at[:, pl.ds(3328, 128)], pool.at[slot, :, pl.ds(0, 128)], slot)
            load(wu.at[:, pl.ds(3328, 128)], pool.at[slot, :, pl.ds(128, 128)], slot)

    def keep_slot(k):
        return RING + lax.rem(k + 5, KEEP)

    def ring_slot(b, l):
        return lax.rem(N_QKV + N_MLP * b + l, RING)

    def load_ring(b, l, lo, hi):
        slot = ring_slot(b, l)

        def g():
            load_g(KEEP + l, slot)

        def d():
            q = l - N_RG
            half = lax.rem(lax.rem(q, 4) // 2 + 1 + core, 2)
            load(wd.at[:, cols(half * 2560 + (q // 4) * 512 + lax.rem(q, 2) * 256, 256)], pool.at[slot, pl.ds(0, 3456), :], slot)

        def nxt():
            load_g(KEEP + l - N_MLP, slot)

        for start, end, fn in ((0, N_RG, g), (N_RG, N_MLP, d), (N_MLP, 2 * N_MLP, nxt if b == 0 else None)):
            if fn is None or hi < start or lo >= end:
                continue
            if lo >= start and hi < end:
                fn()
            else:
                pl.when(jnp.logical_and(l >= start, l < end))(fn)

    def wait_slot(slot, rows=WIDTH):
        src = wq if rows == WIDTH else wd
        pltpu.make_async_copy(src.at[:, pl.ds(0, 256)], pool.at[slot, pl.ds(0, rows), :], wsem.at[slot]).wait()

    def i32(v):
        return jnp.int32(v)

    xcopy = pltpu.make_async_copy(x_hbm, x, xsem)
    xcopy.start()
    for n in range(2):
        load_qk(i32(n))
    small = [pltpu.make_async_copy(src, dst, tsem.at[i]) for i, (src, dst) in enumerate(
        ((cos_hbm, cos_ref), (sin_hbm, sin_ref), (gq_hbm, gq16), (gk_hbm, gk16), (ga_hbm, ga16)))]
    for c in small:
        c.start()
    for n in range(2, 4):
        load_qk(i32(n))

    barrier = pltpu.get_barrier_semaphore()
    for peer in (sib, xpeer, diag):
        pl.semaphore_signal(barrier, inc=1, device_id={"tp": peer}, device_id_type=pl.DeviceIdType.MESH)

    def remote(src, dst, ssem, rsem, peer):
        return pltpu.make_async_remote_copy(src_ref=src, dst_ref=dst, send_sem=ssem, recv_sem=rsem,
                                            device_id={"tp": peer}, device_id_type=pl.DeviceIdType.MESH)

    ssq_acc[...] = jnp.zeros_like(ssq_acc)
    xcopy.wait()

    def qk_step(i, carry):
        n = 2 * i
        s0, s1 = lax.rem(n, RING), lax.rem(n + 1, RING)
        wait_slot(s0)
        wait_slot(s1)
        for m in (n + 4, n + 5):
            pl.when(m < N_V)(lambda m=m: load_qk(m))
            pl.when(m >= N_V)(lambda m=m: load_v(m))
        q = dot(x[...], pool[s0])
        k = dot(x[...], pool[s1])
        for b in range(2):
            for hh in range(2):
                qraw[b, 2 * i + hh] = q[b * 128:(b + 1) * 128, hh * 128:(hh + 1) * 128]
                kraw[b, 2 * i + hh] = k[b * 128:(b + 1) * 128, hh * 128:(hh + 1) * 128]
        ssq_acc[0] += q[:, :128] * q[:, :128] + q[:, 128:] * q[:, 128:]
        ssq_acc[1] += k[:, :128] * k[:, :128] + k[:, 128:] * k[:, 128:]
        return carry

    with jax.named_scope("qk"):
        lax.fori_loop(0, 5, qk_step, 0)

    for r in range(2):
        ssq_send[r:r + 1, :] = jnp.sum(jnp.transpose(ssq_acc[r]), axis=0, keepdims=True)
    ssq_send[2:8, :] = jnp.zeros((6, 256), F32)
    with jax.named_scope("barrier"):
        pl.semaphore_wait(barrier, 3)
    ssq_copies = [remote(ssq_send, ssq_recv.at[j], ssq_s.at[j], ssq_r.at[j], peer) for j, peer in enumerate((sib, xpeer, diag))]
    for c in ssq_copies:
        c.start()

    with jax.named_scope("v"):
        for group in ((10, 11), (12, 13), (14,)):
            for n in group:
                wait_slot(n % RING)
            if group[0] == 10:
                load_v(i32(14))
                load_o(0)
                load_o(1)
            elif group[0] == 12:
                load_o(2)
                load_o(3)
                load_o(4)
            else:
                for k in range(KEEP - 5):
                    load_g(i32(k), keep_slot(i32(k)))
            vals = [dot(x[...], pool[n % RING]).astype(BF16) for n in group]
            for n, v in zip(group, vals):
                for b in range(2):
                    for hh in range(2):
                        vb[b, 2 * (n - N_V) + hh] = v[b * 128:(b + 1) * 128, hh * 128:(hh + 1) * 128]
    vcopy = pltpu.make_async_copy(vb, vc_hbm, csem.at[0])
    vcopy.start()
    for l in range(RING):
        load_ring(0, i32(l), l, l)

    with jax.named_scope("ssqwait"):
        for c in ssq_copies:
            c.wait()
    for c in small:
        c.wait()
    for src, dst in ((gq16, gq_ref), (gk16, gk_ref), (ga16, ga_ref)):
        dst[...] = src[...].astype(F32)
    total = ssq_send[...] + ssq_recv[0] + ssq_recv[1] + ssq_recv[2]
    scale = lax.rsqrt(total * (1.0 / WIDTH) + NORM_EPS)
    for r in range(2):
        rsc[r] = jnp.transpose(jnp.broadcast_to(scale[r:r + 1, :], (128, 256)))

    def rope(v):
        return (v * cos_ref[...] + pltpu.roll(v, 64, 1) * sin_ref[...]).astype(BF16)

    def attention(b):
        rows = pl.ds(b * 128, 128)
        row = lax.broadcasted_iota(jnp.int32, (128, 128), 0)
        col = lax.broadcasted_iota(jnp.int32, (128, 128), 1)
        allowed = jnp.logical_and(col <= row, col < seq_ref[b])
        for h in range(10):
            qb[h] = rope(qraw[b, h] * rsc[0, rows, :] * gq_ref[h:h + 1, :])
            kb[b, h] = rope(kraw[b, h] * rsc[1, rows, :] * gk_ref[h:h + 1, :])
        for h in range(10):
            qraw[b, h] = lax.dot_general(qb[h], kb[b, h], (((1,), (1,)), ((), ())), preferred_element_type=F32)
        for h in range(10):
            s = jnp.where(allowed, qraw[b, h] * HEAD_DIM ** -0.5, -1e30)
            e = jnp.exp(s - jnp.max(s, axis=-1, keepdims=True))
            qb[h] = (e / jnp.sum(e, axis=-1, keepdims=True)).astype(BF16)
        for h in range(10):
            o[rows, pl.ds(h * 128, 128)] = dot(qb[h], vb[b, h]).astype(BF16)

    def rs_copy(p, b, j):
        return remote(rs_send.at[b, j], rs_recv.at[b, j], arsem.at[p, b, 0, j], arsem.at[p, b, 1, j], sib)

    def xs_copy(p, b, j):
        return remote(xs_send.at[b, j], xs_recv.at[p, b, j], arsem.at[p, b, 2, j], arsem.at[p, b, 3, j], xpeer)

    def ag_copy(p, b, j, owner):
        blk = full.at[b, owner * 5 + j]
        return remote(blk, blk, arsem.at[p, b, 4, j], arsem.at[p, b, 5, j], sib)

    def reduce_half(p, b, partial):
        def finish(j):
            rs_copy(p, b, j).wait()
            xs_send[b, j] = (own32[lax.rem(j, 2)] + rs_recv[b, j].astype(F32)).astype(BF16)
            xs_copy(p, b, j).start()

        def step(j, carry):
            parts = partial(j)
            for k in range(2):
                rs_send[b, j, :, pl.ds(k * 256, 256)] = parts[k].astype(BF16)
                own32[lax.rem(j, 2), :, pl.ds(k * 256, 256)] = parts[2 + k]
            rs_copy(p, b, j).start()
            pl.when(j > 0)(lambda: finish(j - 1))
            return carry

        lax.fori_loop(0, 5, step, 0)
        finish(i32(4))

    def squares(b, c):
        v = full[b, c].astype(F32)
        return v[:, :128] * v[:, :128] + v[:, 128:256] * v[:, 128:256] + v[:, 256:384] * v[:, 256:384] + v[:, 384:] * v[:, 384:]

    def gather(p, b):
        sq_acc[b] = jnp.zeros((2, 128, 128), F32)

        def step(j, carry):
            with jax.named_scope(f"xwait{p}{b}"):
                xs_copy(p, b, j).wait()
            full[b, core * 5 + j] = (xs_send[b, j].astype(F32) + xs_recv[p, b, j].astype(F32)).astype(BF16)
            ag_copy(p, b, j, core).start()
            sq_acc[b, 0] += squares(b, core * 5 + j)
            return carry

        lax.fori_loop(0, 5, step, 0)

    def arrive(p, b):
        def step(j, carry):
            ag_copy(p, b, j, core).wait_send()
            ag_copy(p, b, j, 1 - core).wait_recv()
            sq_acc[b, 1] += squares(b, (1 - core) * 5 + j)
            return carry

        lax.fori_loop(0, 5, step, 0)
        rs = lax.rsqrt(jnp.sum(sq_acc[b, 0] + sq_acc[b, 1], axis=-1, keepdims=True) * (1.0 / WIDTH) + NORM_EPS)
        rs_out[p, pl.ds(b * 128, 128), :] = jnp.broadcast_to(rs, (128, 128))

    def norm_hidden(b):
        rows = pl.ds(b * 128, 128)

        def apply(c, carry):
            for w in range(4):
                cs = cols(c * 512 + w * 128, 128)
                x[rows, cs] = (x[rows, cs].astype(F32) + full[b, c, :, pl.ds(w * 128, 128)].astype(F32) * rs_out[0, rows, :] * ga_ref[pl.ds(c * 4 + w, 1), :]).astype(BF16)
            return carry

        lax.fori_loop(0, 10, apply, 0)
        pltpu.make_async_copy(x.at[rows], h_hbm.at[rows], ysem.at[b]).start()

    def o_partial(b):
        def partial(j):
            slot = RING + j
            if b == 0:
                wait_slot(slot)
            return [dot(o[pl.ds(b * 128, 128), :], pool[slot, pl.ds(k * 1280, 1280), :]) for k in range(4)]
        return partial

    for b in range(2):
        with jax.named_scope(f"attn{b}"):
            attention(b)
        with jax.named_scope(f"o{b}"):
            reduce_half(0, b, o_partial(b))
    kcopy = pltpu.make_async_copy(kb, kc_hbm, csem.at[1])
    kcopy.start()
    for k in range(KEEP - 5, KEEP):
        load_g(i32(k), keep_slot(i32(k)))

    def gu_store(i, g, u):
        act[:, cols(i * 256, 256)] = (g * jax.nn.sigmoid(g) * u).astype(BF16)

    def gu_keep(b):
        def step(i, carry):
            s0, s1 = keep_slot(2 * i), keep_slot(2 * i + 1)
            if b == 0:
                wait_slot(s0)
                wait_slot(s1)
            xb = x[pl.ds(b * 128, 128), :]
            gu_store(i, dot(xb, pool[s0]), dot(xb, pool[s1]))
            return carry

        with jax.named_scope(f"gukeep{b}"):
            lax.fori_loop(0, KEEP // 2, step, 0)

    def gu_ring(b):
        def step(i, carry):
            l = 2 * i
            s0, s1 = ring_slot(b, l), ring_slot(b, l + 1)
            wait_slot(s0)
            wait_slot(s1)
            xb = x[pl.ds(b * 128, 128), :]
            gu_store(i + KEEP // 2, dot(xb, pool[s0]), dot(xb, pool[s1]))
            load_ring(b, l + RING, RING, N_RG - 3 + RING)
            load_ring(b, l + 1 + RING, 1 + RING, N_RG - 2 + RING)
            return carry

        with jax.named_scope(f"guring{b}"):
            lax.fori_loop(0, N_RG // 2, step, 0)
        l = N_RG - 1
        s0 = (N_QKV + N_MLP * b + l) % RING
        wait_slot(s0)
        r = dot(x[pl.ds(b * 128, 128), :], pool[s0])
        g = r[:, :128]
        act[:, 3328:3456] = (g * jax.nn.sigmoid(g) * r[:, 128:]).astype(BF16)
        load_ring(b, i32(l + RING), l + RING, l + RING)

    def d_partial(b):
        def partial(j):
            parts = []
            for k in range(4):
                l = N_RG + 4 * j + k
                slot = ring_slot(b, l)
                wait_slot(slot, 3456)
                parts.append(slot)
            parts = [dot(act[...], pool[s, pl.ds(0, 3456), :]) for s in parts]
            for k in range(4):
                l = N_RG + 4 * j + k
                if b == 0:
                    load_ring(b, l + RING, N_RG + RING, N_MLP - 1 + RING)
                else:
                    pl.when(l + RING < N_MLP)(lambda l=l: load_ring(b, l + RING, N_RG + RING, N_MLP - 1))
            return parts
        return partial

    with jax.named_scope("gather00"):
        gather(0, 0)
    with jax.named_scope("norm00"):
        arrive(0, 0)
        norm_hidden(0)
    gu_ring(0)
    gu_keep(0)
    with jax.named_scope("d0"):
        reduce_half(1, 0, d_partial(0))
    with jax.named_scope("gather01"):
        gather(0, 1)
    with jax.named_scope("norm01"):
        arrive(0, 1)
        norm_hidden(1)
    gu_keep(1)
    gu_ring(1)
    with jax.named_scope("d1"):
        reduce_half(1, 1, d_partial(1))
    mcopies = []
    for b in range(2):
        with jax.named_scope(f"gather1{b}"):
            gather(1, b)
        with jax.named_scope(f"arrive1{b}"):
            arrive(1, b)
        mcopies.append(pltpu.make_async_copy(full.at[b], m_hbm.at[b], ysem.at[2 + b]))
        mcopies[-1].start()
    rcopy = pltpu.make_async_copy(rs_out.at[1], rs_hbm, ysem.at[4])
    rcopy.start()
    with jax.named_scope("tail"):
        hcopies = [pltpu.make_async_copy(x.at[pl.ds(b * 128, 128)], h_hbm.at[pl.ds(b * 128, 128)], ysem.at[b]) for b in range(2)]
        for c in [vcopy, kcopy, rcopy] + hcopies + mcopies:
            c.wait()


def finish_kernel(rs_hbm, gm_hbm, h_hbm, m_hbm, k_in, v_in, y_hbm, k_out, v_out, rs, gm, h, m, kb, vb, isem, msem, hsem, osem, ysem):
    copies = [pltpu.make_async_copy(src, dst, isem.at[i]) for i, (src, dst) in enumerate(((rs_hbm, rs), (gm_hbm, gm), (k_in, kb), (v_in, vb)))]
    for c in copies[:2]:
        c.start()

    def inputs(c):
        return [pltpu.make_async_copy(m_hbm.at[:, c], m.at[c], msem.at[c]), pltpu.make_async_copy(h_hbm.at[:, pl.ds(c * 512, 512)], h.at[:, pl.ds(c * 512, 512)], hsem.at[c])]

    for c in range(10):
        for d in inputs(c):
            d.start()
    for c in copies[2:]:
        c.start()
    copies[0].wait()
    copies[1].wait()
    out = []
    for c in range(10):
        for d in inputs(c):
            d.wait()
        for b in range(2):
            rows = pl.ds(b * 128, 128)
            for w in range(4):
                cs = pl.ds(c * 512 + w * 128, 128)
                g = gm[c * 4 + w:c * 4 + w + 1, :].astype(F32)
                h[rows, cs] = (h[rows, cs].astype(F32) + m[c, b, :, pl.ds(w * 128, 128)].astype(F32) * rs[rows, :] * g).astype(BF16)
        cs = pl.ds(c * 512, 512)
        out.append(pltpu.make_async_copy(h.at[:, cs], y_hbm.at[:, cs], ysem.at[c]))
        out[-1].start()
    for i, (src, dst) in enumerate(((kb, k_out), (vb, v_out))):
        copies[2 + i].wait()
        out.append(pltpu.make_async_copy(src, dst, osem.at[i]))
        out[-1].start()
    for d in out:
        d.wait()


def solution(mesh):
    def local_layer(tokens, seq_lens, w_q, w_k, w_v, w_o, g_q, g_k, g_attn, g_mlp, w_gate, w_up, w_down):
        cos_tab, sin_tab = rope_tables(128)
        hbm = pl.BlockSpec(memory_space=pl.ANY)
        gain = lambda g: g.reshape(-1, 128)
        dma = pltpu.SemaphoreType.DMA
        cache = jax.ShapeDtypeStruct((2, 10, 128, 128), BF16)
        hidden = jax.ShapeDtypeStruct((256, 5120), BF16)
        h, m, rs, kc, vc = pl.pallas_call(
            layer_kernel,
            out_shape=(hidden, jax.ShapeDtypeStruct((2, 10, 128, 512), BF16), jax.ShapeDtypeStruct((256, 128), F32), cache, cache),
            in_specs=[pl.BlockSpec(memory_space=pltpu.SMEM)] + [hbm] * 13,
            out_specs=(hbm,) * 5,
            scratch_shapes=[
                pltpu.VMEM((RING + KEEP, 5120, 256), BF16),
                pltpu.VMEM((256, 5120), BF16),
                pltpu.VMEM((2, 10, 128, 128), F32),
                pltpu.VMEM((2, 10, 128, 128), F32),
                pltpu.VMEM((2, 10, 128, 128), BF16),
                pltpu.VMEM((2, 10, 128, 128), BF16),
                pltpu.VMEM((10, 128, 128), BF16),
                pltpu.VMEM((256, 1280), BF16),
                pltpu.VMEM((128, 3456), BF16),
                pltpu.VMEM((2, 128, 512), F32),
                pltpu.VMEM((2, 256, 128), F32),
                pltpu.VMEM((2, 256, 128), F32),
                pltpu.VMEM((8, 256), F32),
                pltpu.VMEM((3, 8, 256), F32),
                pltpu.VMEM((2, 5, 128, 512), BF16),
                pltpu.VMEM((2, 5, 128, 512), BF16),
                pltpu.VMEM((2, 5, 128, 512), BF16),
                pltpu.VMEM((2, 2, 5, 128, 512), BF16),
                pltpu.VMEM((2, 10, 128, 512), BF16),
                pltpu.VMEM((2, 2, 128, 128), F32),
                pltpu.VMEM((2, 256, 128), F32),
                pltpu.VMEM((128, 128), F32),
                pltpu.VMEM((128, 128), F32),
                pltpu.VMEM((10, 128), BF16),
                pltpu.VMEM((10, 128), BF16),
                pltpu.VMEM((40, 128), BF16),
                pltpu.VMEM((10, 128), F32),
                pltpu.VMEM((10, 128), F32),
                pltpu.VMEM((40, 128), F32),
                dma((RING + KEEP,)), dma, dma((2,)), dma((5,)), dma((3,)), dma((3,)), dma((2, 2, 6, 5)), dma((5,)),
            ],
            compiler_params=pltpu.CompilerParams(collective_id=0, has_side_effects=True, vmem_limit_bytes=67043328),
        )(seq_lens, jnp.asarray(cos_tab), jnp.asarray(sin_tab), gain(g_q), gain(g_k), gain(g_attn),
          tokens.reshape(256, 5120), w_q, w_k, w_v, w_o, w_gate, w_up, w_down)
        y, kc, vc = pl.pallas_call(
            finish_kernel,
            out_shape=(hidden, cache, cache),
            in_specs=[hbm] * 6,
            out_specs=(hbm,) * 3,
            scratch_shapes=[
                pltpu.VMEM((256, 128), F32),
                pltpu.VMEM((40, 128), BF16),
                pltpu.VMEM((256, 5120), BF16),
                pltpu.VMEM((10, 2, 128, 512), BF16),
                pltpu.VMEM((2, 10, 128, 128), BF16),
                pltpu.VMEM((2, 10, 128, 128), BF16),
                dma((4,)), dma((10,)), dma((10,)), dma((2,)), dma((10,)),
            ],
            compiler_params=pltpu.CompilerParams(vmem_limit_bytes=60000000),
        )(rs, gain(g_mlp), h, m, kc, vc)
        return y.reshape(2, 128, 5120), kc, vc

    return jax.shard_map(local_layer, mesh=mesh, in_specs=(P('dp', None, None), P('dp'), P(None, 'tp'), P(None, 'tp'), P(None, 'tp'), P('tp', None), P('tp'), P('tp'), P(), P(), P(None, 'tp'), P(None, 'tp'), P('tp', None)), out_specs=(P('dp', None, None), P('dp', 'tp', None, None), P('dp', 'tp', None, None)), check_vma=False)
```

time: 237 us -> 112 us (0.47)
  Pallas kernels: 0 us -> 111 us
  waiting for transfers between devices: 109 us -> 0 us
  matrix products: 79.7 us -> 0 us
  other arithmetic: 16.9 us -> 0 us
  between operations: 14.2 us -> 0.8 us
  local copies, waits for them, and re-layouts: 8.66 us -> 0 us
  blocking collectives: 8.61 us -> 0 us
    pallas_call x0 -> x2, Pallas kernels: none -> 111 us  [the longest x1 107 us: local_layer(): pl.pallas_call(layer_kernel, out_shape=(hidden, jax.ShapeDtypeStruct((2,...]
    psum x2 -> x0, waiting for transfers between devices: 109 us -> none  [the longest x1 55.6 us: local_layer(): attn_proj = lax.psum(attn_part, 'tp')]
    dot_general x8 -> x0, matrix products: 79.7 us -> none  [the longest x1 30.1 us: local_layer(): jnp.einsum('bsf,fd->bsd', act_out, w_down, preferred_element_type=jnp.flo...]
    psum x1 -> x0, blocking collectives: 8.61 us -> none  [local_layer(): k_sumsq = lax.psum(jnp.sum(k_raw * k_raw, axis=-1, keepdims=True), 'tp')]
    convert_element_type x6 -> x0, other arithmetic: 5.88 us -> none  [the longest x2 5.86 us: post_norm(): (base.astype(jnp.float32) + branch32 * rms_scale(branch32) * gain.astype(...]
    unnamed x30 -> x0, local copies, waits for them, and re-layouts: 5.46 us -> none
    reduce_sum x3 -> x0, other arithmetic: 5.17 us -> none  [the longest x2 4.98 us: rms_scale(): return lax.rsqrt(jnp.mean(vals * vals, axis=-1, keepdims=True) + NORM_EPS)]
  transfers between devices with their start and end apart: 2 -> 0, of which waited for: 2 -> 0; matrix products, arithmetic and copies ran while one was open for 1% -> 0% of each run, Pallas kernels for 0% -> 0%
where the time goes in v3:
time: 112 us
  Pallas kernels  111 us (99%)
    pallas_call x1, Pallas kernels, local_layer(): pl.pallas_call(layer_kernel, out_shape=(hidden, jax.ShapeDtypeStruct((2,...  107 us
    pallas_call x1, Pallas kernels, local_layer(): pl.pallas_call(finish_kernel, out_shape=(hidden, cache, cache), in_specs=...  4.5 us

profile of v3, /device:TPU:0, one launch (start us, length us, event | category | flops | bytes accessed | tf_op | source)
XLA Modules:
  0.0 112.1 jit_solution(10394595374140061990)
XLA Ops:
  0.6 106.8 %shard_map.166 = (bf16[256,5120]{1,0:T(8,128)(2,1)}, bf16[2,10,128,512]{3,2,1,0:T(8,128)(2,1)}, f32[256,128]{1,0:T(8,128)}, bf16[2,10,128,128]{3,2,1,0:T(8,128)(2,1)}, bf16[2,10,128,128]{3,2,1,0:T(8,128)(2,1)}) custom-call(s32[2]{0:T(128)} %seq_ref.1, f32[128,128]{1,0:T(8,128)} %constant.4.clone.cos_hbm, f32[128,128]{1,0:T(8,128)} %constant.5.clone.sin_hbm, ...), custom_call_target="tpu_custom_call" | custom-call | tf_op jit(solution)/shard_map/pallas_call | solution.py:455
  107.5 4.5 %shard_map.167 = (bf16[256,5120]{1,0:T(8,128)(2,1)}, bf16[2,10,128,128]{3,2,1,0:T(8,128)(2,1)}, bf16[2,10,128,128]{3,2,1,0:T(8,128)(2,1)}) custom-call(f32[256,128]{1,0:T(8,128)} %get-tuple-element.11.rs_hbm, bf16[40,128]{1,0:T(8,128)(2,1)} %bitcast.8, bf16[256,5120]{1,0:T(8,128)(2,1)} %get-tuple-element.12.h_hbm, ...), custom_call_target="tpu_custom_call" | custom-call | tf_op jit(solution)/shard_map/pallas_call | solution.py:495
